TPU v7x, 32 devices: a whole 2x2x4 slice. The times are simulated.
32 devices in a mesh: row: 8 (over z, y), col: 4 (over x, core).
Axes of the slice: x: 2, y: 2, z: 4, core: 2. Of those that a mesh axis runs over, the one named last changes fastest.
Arguments:
- matrix: float32 [4096, 4096], P('row', 'col'), may hold values from -0.92 to 1.92, as said below
Outputs:
- inverse: float32 [4096, 4096], P('row', 'col')
- residual_norms: float32 [4], replicated
Inputs may be any that keep to these rules, and one draw needn't show every extreme that they name: matrix is exactly symmetric and positive definite; all its eigenvalues lie between 0.08 and 1.92.
All inputs are finite; a program needn't handle non-finite values.
Results may differ from a plain program's by a relative error of at most 0.0017.
The roundings to bfloat16 on the way count: a program that leaves them out, or rounds other values in their place, can miss the bound.
Values may be sent and summed in bfloat16 or wider, within the bound.
A program may use at most 64 MiB of HBM per device.

v0:
```python
import jax
import jax.numpy as jnp
from jax import lax
from jax.sharding import PartitionSpec as P

ITERS = 4


def rounded(value):
    return lax.reduce_precision(value, 8, 7)


def first_iterate(panel, scale_low, row_start, col_start):
    rows = row_start + lax.broadcasted_iota(jnp.int32, panel.shape, 0)
    cols = col_start + lax.broadcasted_iota(jnp.int32, panel.shape, 1)
    eye = (rows == cols).astype(jnp.float32)
    shift = rounded(eye + (eye - scale_low * panel.astype(jnp.float32)))
    return (scale_low * shift).astype(jnp.bfloat16)


def transpose_blocks(block, row_size, col_size):
    ratio = row_size // col_size
    side = block.shape[0]
    row_index = lax.axis_index("row")
    pieces = []
    for turn in range(ratio):
        pairs = []
        for row in range(row_size):
            for col in range(col_size):
                target_row = ratio * col + (row + turn) % ratio
                pairs.append((row * col_size + col, target_row * col_size + row // ratio))
        half = lax.rem(row_index + turn, ratio)
        piece = lax.dynamic_slice_in_dim(block, half * side, side, axis=1)
        pieces.append(lax.ppermute(piece, ("row", "col"), pairs).T)
    out = jnp.zeros_like(block)
    for turn in range(ratio):
        half = lax.rem(row_index - turn + ratio, ratio)
        out = lax.dynamic_update_slice_in_dim(out, pieces[turn], half * side, axis=1)
    return out


def shards(matrix):
    row_count, col_count = matrix.shape
    row_size, col_size = (lax.axis_size("row"), lax.axis_size("col"))
    order = col_count * col_size
    row_start = lax.axis_index("row") * row_count
    col_start = lax.axis_index("col") * col_count
    global_rows = row_start + lax.broadcasted_iota(jnp.int32, (row_count, col_count), 0)
    global_cols = col_start + lax.broadcasted_iota(jnp.int32, (row_count, col_count), 1)
    eye_block = (global_rows == global_cols).astype(jnp.float32)
    mat_low = matrix.astype(jnp.bfloat16)
    sq_total = lax.psum(jnp.sum(matrix * matrix), ("row", "col"))
    panel_rows = lax.all_gather(mat_low, "col", axis=1, tiled=True)
    panel_cols = lax.all_gather(mat_low, "row", axis=0, tiled=True)
    start_scale = jnp.sqrt(jnp.float32(order)) / jnp.sqrt(sq_total)
    scale_low = rounded(start_scale)
    residual = eye_block - scale_low * rounded(matrix)
    partial_list = [jnp.sum(residual * residual)]
    iterate_rows = first_iterate(panel_rows, scale_low, row_start, 0)
    iterate_cols = first_iterate(panel_cols, scale_low, 0, col_start)
    for iteration in range(1, ITERS):
        product = jnp.dot(iterate_rows, panel_cols, preferred_element_type=jnp.float32)
        residual = eye_block - product
        partial_list.append(jnp.sum(residual * residual))
        shift_low = (eye_block + residual).astype(jnp.bfloat16)
        current = jnp.dot(
            lax.all_gather(shift_low, "col", axis=1, tiled=True),
            iterate_cols,
            preferred_element_type=jnp.float32,
        )
        if iteration < ITERS - 1:
            cur_low = current.astype(jnp.bfloat16)
            iterate_rows = lax.all_gather(cur_low, "col", axis=1, tiled=True)
            iterate_cols = lax.all_gather(cur_low, "row", axis=0, tiled=True)
    summed = lax.psum(jnp.stack(partial_list), ("row", "col"))
    residual_norms = jnp.sqrt(summed / order)
    return (transpose_blocks(current, row_size, col_size), residual_norms)


def solution(mesh):
    in_specs = (P("row", "col"),)
    out_specs = (P("row", "col"), P())
    return jax.shard_map(shards, mesh=mesh, in_specs=in_specs, out_specs=out_specs, check_vma=False)
```

profile of v0, /device:TPU:0, one launch (start us, length us, event | category | flops | bytes accessed | tf_op | source)
XLA Modules:
  0.0 790.7 jit_solution(10998236796299218012)
XLA Ops:
  7.2 4.3 multiply_reduce_fusion.3
  11.5 0.7 all-gather.12.cloned.1.call-update
  12.3 42.5 %psum.14 = f32[]{:T(128)} all-reduce(f32[]{:T(128)} %get-tuple-element.9), channel_id=1, replica_groups=mesh['row'=8,'col'=4] {'row','col'}, use_global_device_ids=true, to_apply=%region_1.0 | all-reduce | flops 1 | bytes 8 | tf_op jit(solution)/shard_map/psum | solution.py:52
  56.0 120.3 %all-gather.12.cloned.1.call-done = bf16[4096,1024]{1,0:T(8,128)(2,1)} async-done(((bf16[512,1024]{1,0:T(8,128)(2,1)}), bf16[4096,1024]{1,0:T(8,128)(2,1)}) %all-gather.12.cloned.1.call-update) | async-done | bytes 8388624 | tf_op jit(solution)/shard_map/all_gather | solution.py:54
  176.3 12.1 %fusion.12 = (bf16[512,1024]{1,0:T(8,128)(2,1)}, f32[512,1024]{1,0:T(8,128)}) fusion(s32[1024]{0:T(1024)S(1)} %iota_add_fusion, s32[512]{0:T(512)S(1)} %iota_add_fusion.1, bf16[4096,1024]{1,0:T(8,128)(2,1)} %all-gather.12.cloned.1.call-done, bf16[512,4096]{1,0:T(8,128)(2,1)} %all-gather.10.cloned.1.call-done, f32[]{:T(128)} %reduce_precision.12), kind=kOutput, calls=%fused_computation.21 | convolution fusion | flops 4316463104 | bytes 15734788 | tf_op jit(solution)/shard_map/dot_general | solution.py:62
  188.5 32.7 %all-gather.14.cloned.1.call-done = bf16[512,4096]{1,0:T(8,128)(2,1)} async-done(((bf16[512,1024]{1,0:T(8,128)(2,1)}), bf16[512,4096]{1,0:T(8,128)(2,1)}) %all-gather.14.cloned.1.call-update) | async-done | bytes 4194320 | tf_op jit(solution)/shard_map/all_gather | solution.py:67
  221.3 12.0 %fusion.17 = bf16[512,1024]{1,0:T(8,128)(2,1)} fusion(bf16[512,4096]{1,0:T(8,128)(2,1)} %all-gather.14.cloned.1.call-done, bf16[4096,1024]{1,0:T(8,128)(2,1)} %all-gather.12.cloned.1.call-done, s32[1024]{0:T(1024)S(1)} %iota_add_fusion, f32[]{:T(128)} %reduce_precision.12), kind=kOutput, calls=%fused_computation.30 | convolution fusion | flops 4333240320 | bytes 13635588 | tf_op jit(solution)/shard_map/dot_general | solution.py:66
  233.3 0.2 all-gather.18.cloned.1.call-start
  233.5 34.4 %all-gather.16.cloned.1.call-done = bf16[512,4096]{1,0:T(8,128)(2,1)} async-done(((bf16[512,1024]{1,0:T(8,128)(2,1)}), bf16[512,4096]{1,0:T(8,128)(2,1)}) %all-gather.16.cloned.1.call-update) | async-done | bytes 4194320 | tf_op jit(solution)/shard_map/all_gather | solution.py:73
  267.9 10.9 %fusion.13 = (bf16[512,1024]{1,0:T(8,128)(2,1)}, f32[512,1024]{1,0:T(8,128)}) fusion(s32[1024]{0:T(1024)S(1)} %iota_add_fusion, s32[512]{0:T(512)S(1)} %iota_add_fusion.1, bf16[512,4096]{1,0:T(8,128)(2,1)} %all-gather.16.cloned.1.call-done, bf16[4096,1024]{1,0:T(8,128)(2,1)} %all-gather.12.cloned.1.call-done), kind=kOutput, calls=%fused_computation.22 | convolution fusion | flops 4297588736 | bytes 15734784 | tf_op jit(solution)/shard_map/dot_general | solution.py:62
  278.8 0.5 all-gather.20.cloned.1.call-update
  279.4 34.0 %all-gather.18.cloned.1.call-done = bf16[512,4096]{1,0:T(8,128)(2,1)} async-done(((bf16[512,1024]{1,0:T(8,128)(2,1)}), bf16[512,4096]{1,0:T(8,128)(2,1)}) %all-gather.18.cloned.1.call-update) | async-done | bytes 4194320 | tf_op jit(solution)/shard_map/all_gather | solution.py:67
  313.4 126.5 %all-gather.20.cloned.1.call-done = bf16[4096,1024]{1,0:T(8,128)(2,1)} async-done(((bf16[512,1024]{1,0:T(8,128)(2,1)}), bf16[4096,1024]{1,0:T(8,128)(2,1)}) %all-gather.20.cloned.1.call-update) | async-done | bytes 8388624 | tf_op jit(solution)/shard_map/all_gather | solution.py:74
  439.9 10.2 %convolution_convert_fusion = bf16[512,1024]{1,0:T(8,128)(2,1)} fusion(bf16[512,4096]{1,0:T(8,128)(2,1)} %all-gather.18.cloned.1.call-done, bf16[4096,1024]{1,0:T(8,128)(2,1)} %all-gather.20.cloned.1.call-done), kind=kOutput, calls=%fused_computation.31 | convolution fusion | flops 4295491584 | bytes 13631488 | tf_op jit(solution)/shard_map/dot_general | solution.py:66
  450.1 32.7 %all-gather.22.cloned.1.call-done = bf16[512,4096]{1,0:T(8,128)(2,1)} async-done(((bf16[512,1024]{1,0:T(8,128)(2,1)}), bf16[512,4096]{1,0:T(8,128)(2,1)}) %all-gather.22.cloned.1.call-update) | async-done | bytes 4194320 | tf_op jit(solution)/shard_map/all_gather | solution.py:73
  482.8 13.2 %fusion.16 = (f32[]{:T(128)}, f32[]{:T(128)}, f32[]{:T(128)}, f32[]{:T(128)}, bf16[512,1024]{1,0:T(8,128)(2,1)}) fusion(f32[512,1024]{1,0:T(8,128)S(1)} %copy-done.1, f32[]{:T(128)} %reduce_precision.12, s32[1024]{0:T(1024)S(1)} %iota_add_fusion, s32[512]{0:T(512)S(1)} %iota_add_fusion.1, f32[512,1024]{1,0:T(8,128)} %get-tuple-element.14, ...), kind=kOutput, calls=%fused_computation.25 | convolution fusion | flops 4304404480 | bytes 19929108 | tf_op jit(solution)/shard_map/dot_general | solution.py:62
  496.0 0.3 all-gather.26.cloned.1.call-start
  496.3 0.5 all-gather.26.cloned.1.call-update
  496.8 33.9 %all-gather.24.cloned.1.call-done = bf16[512,4096]{1,0:T(8,128)(2,1)} async-done(((bf16[512,1024]{1,0:T(8,128)(2,1)}), bf16[512,4096]{1,0:T(8,128)(2,1)}) %all-gather.24.cloned.1.call-update) | async-done | bytes 4194320 | tf_op jit(solution)/shard_map/all_gather | solution.py:67
  530.6 126.6 %all-gather.26.cloned.1.call-done = bf16[4096,1024]{1,0:T(8,128)(2,1)} async-done(((bf16[512,1024]{1,0:T(8,128)(2,1)}), bf16[4096,1024]{1,0:T(8,128)(2,1)}) %all-gather.26.cloned.1.call-update) | async-done | bytes 8388624 | tf_op jit(solution)/shard_map/all_gather | solution.py:74
  657.3 8.1 %fusion.20 = f32[512,1024]{1,0:T(8,128)S(1)} fusion(bf16[512,4096]{1,0:T(8,128)(2,1)} %all-gather.24.cloned.1.call-done, bf16[4096,1024]{1,0:T(8,128)(2,1)} %all-gather.26.cloned.1.call-done), kind=kOutput, calls=%fused_computation.40 | convolution fusion | flops 4294967296 | bytes 14680064 | tf_op jit(solution)/shard_map/dot_general | solution.py:66
  665.4 0.2 constant_dynamic-slice_fusion
  665.7 1.6 collective-permute-start
  667.3 0.6 collective-permute-start.1
  667.8 2.5 pad_maximum_fusion
  670.4 109.5 %psum.15 = f32[4]{0:T(128)S(1)} all-reduce(f32[4]{0:T(128)S(1)} %pad_maximum_fusion), channel_id=1, replica_groups=mesh['row'=8,'col'=4] {'row','col'}, use_global_device_ids=true, to_apply=%region_6.0 | all-reduce | flops 4 | bytes 32 | tf_op jit(solution)/shard_map/psum | solution.py:75
  779.9 0.5 multiply_sqrt_fusion
  780.4 1.6 copy.3
  782.0 0.3 copy.4
  782.4 0.2 broadcast_in_dim.3
  782.6 0.1 constant_dynamic-update-slice_fusion.1
  782.8 1.3 copy-done
  (22 shorter events, 0.5 us)
Async XLA Ops:
  7.2 48.9 %all-gather.10.cloned.1.call-start = ((), (), s32[]{:S(2)}) async-start(), calls=%async_computation | async-start | bytes 5242880 | tf_op jit(solution)/shard_map/all_gather | solution.py:53
  11.5 164.8 %all-gather.12.cloned.1.call-start = ((), (), s32[]{:S(2)}) async-start(), calls=%async_computation.1 | async-start | bytes 9437184 | tf_op jit(solution)/shard_map/all_gather | solution.py:54
  12.3 209.0 %all-gather.14.cloned.1.call-start = ((), (), s32[]{:S(2)}) async-start(), calls=%async_computation.2 | async-start | bytes 5242880 | tf_op jit(solution)/shard_map/all_gather | solution.py:67
  188.5 79.4 %all-gather.16.cloned.1.call-start = ((), (), s32[]{:S(2)}) async-start(), calls=%async_computation.3 | async-start | bytes 5242880 | tf_op jit(solution)/shard_map/all_gather | solution.py:73
  233.3 80.1 %all-gather.18.cloned.1.call-start = ((), (), s32[]{:S(2)}) async-start(), calls=%async_computation.4 | async-start | bytes 5242880 | tf_op jit(solution)/shard_map/all_gather | solution.py:67
  278.8 161.1 %all-gather.20.cloned.1.call-start = ((), (), s32[]{:S(2)}) async-start(), calls=%async_computation.5 | async-start | bytes 9437184 | tf_op jit(solution)/shard_map/all_gather | solution.py:74
  279.3 203.5 %copy-start.1 = (f32[512,1024]{1,0:T(8,128)S(1)}, f32[512,1024]{1,0:T(8,128)}, u32[]{:S(2)}) copy-start(f32[512,1024]{1,0:T(8,128)} %param.1) | copy-start | bytes 6291460
  279.4 203.5 %all-gather.22.cloned.1.call-start = ((), (), s32[]{:S(2)}) async-start(), calls=%async_computation.6 | async-start | bytes 5242880 | tf_op jit(solution)/shard_map/all_gather | solution.py:73
  450.1 80.6 %all-gather.24.cloned.1.call-start = ((), (), s32[]{:S(2)}) async-start(), calls=%async_computation.7 | async-start | bytes 5242880 | tf_op jit(solution)/shard_map/all_gather | solution.py:67
  496.0 161.3 %all-gather.26.cloned.1.call-start = ((), (), s32[]{:S(2)}) async-start(), calls=%async_computation.8 | async-start | bytes 9437184 | tf_op jit(solution)/shard_map/all_gather | solution.py:74
  665.7 114.8 %collective-permute-start = (f32[512,512]{1,0:T(8,128)S(1)}, f32[512,512]{1,0:T(8,128)}, u32[]{:S(2)}, u32[]{:S(2)}) collective-permute-start(f32[512,512]{1,0:T(8,128)S(1)} %get-tuple-element.8), channel_id=1, source_target_pairs={{0,0},{1,8},{2,16},{3,24},{4,4},{5,12},{6,20},{7,28},{8,1},{9,9},{... | collective-permute-start | bytes 3145736 | tf_op jit(solution)/shard_map/ppermute | solution.py:34
  667.3 114.7 %collective-permute-start.1 = (f32[512,512]{1,0:T(8,128)S(1)}, f32[512,512]{1,0:T(8,128)S(1)}, u32[]{:S(2)}, u32[]{:S(2)}) collective-permute-start(f32[512,512]{1,0:T(8,128)S(1)} %get-tuple-element.7), channel_id=1, source_target_pairs={{0,4},{1,12},{2,20},{3,28},{4,0},{5,8},{6,16},{7,24},{8,5},{9,13},... | collective-permute-start | bytes 3145736 | tf_op jit(solution)/shard_map/ppermute | solution.py:34
  782.8 1.3 copy-start
Sparse Core Ops, SparseCore 0:
  11.6 37.4 all-gather.9
  51.8 124.4 all-gather.11
  188.6 32.6 all-gather.13
  233.4 34.4 all-gather.15
  278.9 34.4 all-gather.17
  315.4 124.4 all-gather.19
  450.2 32.6 all-gather.21
  496.1 34.4 all-gather.23
  532.8 124.4 all-gather.25
where the time goes:
time: 791 us
  waiting for transfers between devices  543 us (69%)
  blocking collectives  152 us (19%)
  matrix products  66.4 us (8%)
  between operations  15.1 us (2%)
    all_gather x2, waiting for transfers between devices, shards(): iterate_cols = lax.all_gather(cur_low, 'row', axis=0, tiled=True)  253 us
    all_gather x1, waiting for transfers between devices, shards(): panel_cols = lax.all_gather(mat_low, 'row', axis=0, tiled=True)  120 us
    psum x1, blocking collectives, shards(): summed = lax.psum(jnp.stack(partial_list), ('row', 'col'))  110 us
    all_gather x3, waiting for transfers between devices, shards(): lax.all_gather(shift_low, 'col', axis=1, tiled=True)  101 us
    all_gather x2, waiting for transfers between devices, shards(): iterate_rows = lax.all_gather(cur_low, 'col', axis=1, tiled=True)  67.1 us
    psum x1, blocking collectives, shards(): sq_total = lax.psum(jnp.sum(matrix * matrix), ('row', 'col'))  42.5 us
    dot_general x3, matrix products, shards(): jnp.dot(iterate_rows, panel_cols, preferred_element_type=jnp.float32)  36.2 us
    dot_general x3, matrix products, shards(): jnp.dot(lax.all_gather(shift_low, 'col', axis=1, tiled=True), iterate_col...  30.3 us
  transfers between devices with their start and end apart: 11, of which 8 were waited for; matrix products, arithmetic and copies ran while one was open for 1% of the time, Pallas kernels for 0%

commit v1 on v0

--- a/solution.py
+++ b/solution.py
@@ -72,7 +72,9 @@
             cur_low = current.astype(jnp.bfloat16)
             iterate_rows = lax.all_gather(cur_low, "col", axis=1, tiled=True)
             iterate_cols = lax.all_gather(cur_low, "row", axis=0, tiled=True)
-    summed = lax.psum(jnp.stack(partial_list), ("row", "col"))
+    summed = jnp.stack(partial_list)
+    for name in ("col", "row"):
+        summed = lax.psum(summed, name)
     residual_norms = jnp.sqrt(summed / order)
     return (transpose_blocks(current, row_size, col_size), residual_norms)
 

time: 791 us -> 778 us (0.984)
  the two profiles are of different devices: /device:TPU:0 before, /device:TPU:8 now
where the time goes in v1:
time: 778 us
  waiting for transfers between devices  541 us (70%)
  blocking collectives  139 us (18%)
  matrix products  66.4 us (9%)
  between operations  15.2 us (2%)
    all_gather x2, waiting for transfers between devices, shards(): iterate_cols = lax.all_gather(cur_low, 'row', axis=0, tiled=True)  249 us
    all_gather x1, waiting for transfers between devices, shards(): panel_cols = lax.all_gather(mat_low, 'row', axis=0, tiled=True)  118 us
    all_gather x3, waiting for transfers between devices, shards(): lax.all_gather(shift_low, 'col', axis=1, tiled=True)  102 us
    psum x2, blocking collectives, shards(): summed = lax.psum(summed, name)  98.3 us
    all_gather x2, waiting for transfers between devices, shards(): iterate_rows = lax.all_gather(cur_low, 'col', axis=1, tiled=True)  69 us
    psum x1, blocking collectives, shards(): sq_total = lax.psum(jnp.sum(matrix * matrix), ('row', 'col'))  41 us
    dot_general x3, matrix products, shards(): jnp.dot(iterate_rows, panel_cols, preferred_element_type=jnp.float32)  36.2 us
    dot_general x3, matrix products, shards(): jnp.dot(lax.all_gather(shift_low, 'col', axis=1, tiled=True), iterate_col...  30.2 us
  transfers between devices with their start and end apart: 11, of which 8 were waited for; matrix products, arithmetic and copies ran while one was open for 1% of the time, Pallas kernels for 0%

profile of v1, /device:TPU:8, one launch (start us, length us, event | category | flops | bytes accessed | tf_op | source)
XLA Modules:
  0.0 777.6 jit_solution(14560147434031521570)
XLA Ops:
  7.2 4.3 multiply_reduce_fusion.3
  11.5 0.7 all-gather.12.cloned.1.call-update
  12.3 41.0 %psum.21 = f32[]{:T(128)} all-reduce(f32[]{:T(128)} %get-tuple-element.9), channel_id=1, replica_groups=mesh['row'=8,'col'=4] {'row','col'}, use_global_device_ids=true, to_apply=%region_1.0 | all-reduce | flops 1 | bytes 8 | tf_op jit(solution)/shard_map/psum | solution.py:52
  54.5 118.4 %all-gather.12.cloned.1.call-done = bf16[4096,1024]{1,0:T(8,128)(2,1)} async-done(((bf16[512,1024]{1,0:T(8,128)(2,1)}), bf16[4096,1024]{1,0:T(8,128)(2,1)}) %all-gather.12.cloned.1.call-update) | async-done | bytes 8388624 | tf_op jit(solution)/shard_map/all_gather | solution.py:54
  172.9 12.1 %fusion.12 = (bf16[512,1024]{1,0:T(8,128)(2,1)}, f32[512,1024]{1,0:T(8,128)}) fusion(s32[1024]{0:T(1024)S(1)} %iota_add_fusion, s32[512]{0:T(512)S(1)} %iota_add_fusion.1, bf16[4096,1024]{1,0:T(8,128)(2,1)} %all-gather.12.cloned.1.call-done, bf16[512,4096]{1,0:T(8,128)(2,1)} %all-gather.10.cloned.1.call-done, f32[]{:T(128)} %reduce_precision.12), kind=kOutput, calls=%fused_computation.21 | convolution fusion | flops 4316463104 | bytes 15734788 | tf_op jit(solution)/shard_map/dot_general | solution.py:62
  185.1 34.6 %all-gather.14.cloned.1.call-done = bf16[512,4096]{1,0:T(8,128)(2,1)} async-done(((bf16[512,1024]{1,0:T(8,128)(2,1)}), bf16[512,4096]{1,0:T(8,128)(2,1)}) %all-gather.14.cloned.1.call-update) | async-done | bytes 4194320 | tf_op jit(solution)/shard_map/all_gather | solution.py:67
  219.7 11.9 %fusion.17 = bf16[512,1024]{1,0:T(8,128)(2,1)} fusion(bf16[512,4096]{1,0:T(8,128)(2,1)} %all-gather.14.cloned.1.call-done, bf16[4096,1024]{1,0:T(8,128)(2,1)} %all-gather.12.cloned.1.call-done, s32[1024]{0:T(1024)S(1)} %iota_add_fusion, f32[]{:T(128)} %reduce_precision.12), kind=kOutput, calls=%fused_computation.30 | convolution fusion | flops 4333240320 | bytes 13635588 | tf_op jit(solution)/shard_map/dot_general | solution.py:66
  231.7 0.2 all-gather.18.cloned.1.call-start
  231.9 34.4 %all-gather.16.cloned.1.call-done = bf16[512,4096]{1,0:T(8,128)(2,1)} async-done(((bf16[512,1024]{1,0:T(8,128)(2,1)}), bf16[512,4096]{1,0:T(8,128)(2,1)}) %all-gather.16.cloned.1.call-update) | async-done | bytes 4194320 | tf_op jit(solution)/shard_map/all_gather | solution.py:73
  266.3 10.9 %fusion.13 = (bf16[512,1024]{1,0:T(8,128)(2,1)}, f32[512,1024]{1,0:T(8,128)}) fusion(s32[1024]{0:T(1024)S(1)} %iota_add_fusion, s32[512]{0:T(512)S(1)} %iota_add_fusion.1, bf16[512,4096]{1,0:T(8,128)(2,1)} %all-gather.16.cloned.1.call-done, bf16[4096,1024]{1,0:T(8,128)(2,1)} %all-gather.12.cloned.1.call-done), kind=kOutput, calls=%fused_computation.22 | convolution fusion | flops 4297588736 | bytes 15734784 | tf_op jit(solution)/shard_map/dot_general | solution.py:62
  277.2 0.5 all-gather.20.cloned.1.call-update
  277.8 34.0 %all-gather.18.cloned.1.call-done = bf16[512,4096]{1,0:T(8,128)(2,1)} async-done(((bf16[512,1024]{1,0:T(8,128)(2,1)}), bf16[512,4096]{1,0:T(8,128)(2,1)}) %all-gather.18.cloned.1.call-update) | async-done | bytes 4194320 | tf_op jit(solution)/shard_map/all_gather | solution.py:67
  311.8 124.6 %all-gather.20.cloned.1.call-done = bf16[4096,1024]{1,0:T(8,128)(2,1)} async-done(((bf16[512,1024]{1,0:T(8,128)(2,1)}), bf16[4096,1024]{1,0:T(8,128)(2,1)}) %all-gather.20.cloned.1.call-update) | async-done | bytes 8388624 | tf_op jit(solution)/shard_map/all_gather | solution.py:74
  436.4 10.1 %convolution_convert_fusion = bf16[512,1024]{1,0:T(8,128)(2,1)} fusion(bf16[512,4096]{1,0:T(8,128)(2,1)} %all-gather.18.cloned.1.call-done, bf16[4096,1024]{1,0:T(8,128)(2,1)} %all-gather.20.cloned.1.call-done), kind=kOutput, calls=%fused_computation.31 | convolution fusion | flops 4295491584 | bytes 13631488 | tf_op jit(solution)/shard_map/dot_general | solution.py:66
  446.6 34.6 %all-gather.22.cloned.1.call-done = bf16[512,4096]{1,0:T(8,128)(2,1)} async-done(((bf16[512,1024]{1,0:T(8,128)(2,1)}), bf16[512,4096]{1,0:T(8,128)(2,1)}) %all-gather.22.cloned.1.call-update) | async-done | bytes 4194320 | tf_op jit(solution)/shard_map/all_gather | solution.py:73
  481.2 13.2 %fusion.16 = (f32[]{:T(128)}, f32[]{:T(128)}, f32[]{:T(128)}, f32[]{:T(128)}, bf16[512,1024]{1,0:T(8,128)(2,1)}) fusion(f32[512,1024]{1,0:T(8,128)S(1)} %copy-done.1, f32[]{:T(128)} %reduce_precision.12, s32[1024]{0:T(1024)S(1)} %iota_add_fusion, s32[512]{0:T(512)S(1)} %iota_add_fusion.1, f32[512,1024]{1,0:T(8,128)} %get-tuple-element.14, ...), kind=kOutput, calls=%fused_computation.25 | convolution fusion | flops 4304404480 | bytes 19929108 | tf_op jit(solution)/shard_map/dot_general | solution.py:62
  494.4 0.3 all-gather.26.cloned.1.call-start
  494.7 0.5 all-gather.26.cloned.1.call-update
  495.2 33.9 %all-gather.24.cloned.1.call-done = bf16[512,4096]{1,0:T(8,128)(2,1)} async-done(((bf16[512,1024]{1,0:T(8,128)(2,1)}), bf16[512,4096]{1,0:T(8,128)(2,1)}) %all-gather.24.cloned.1.call-update) | async-done | bytes 4194320 | tf_op jit(solution)/shard_map/all_gather | solution.py:67
  529.0 124.8 %all-gather.26.cloned.1.call-done = bf16[4096,1024]{1,0:T(8,128)(2,1)} async-done(((bf16[512,1024]{1,0:T(8,128)(2,1)}), bf16[4096,1024]{1,0:T(8,128)(2,1)}) %all-gather.26.cloned.1.call-update) | async-done | bytes 8388624 | tf_op jit(solution)/shard_map/all_gather | solution.py:74
  653.8 8.1 %fusion.20 = f32[512,1024]{1,0:T(8,128)S(1)} fusion(bf16[512,4096]{1,0:T(8,128)(2,1)} %all-gather.24.cloned.1.call-done, bf16[4096,1024]{1,0:T(8,128)(2,1)} %all-gather.26.cloned.1.call-done), kind=kOutput, calls=%fused_computation.40 | convolution fusion | flops 4294967296 | bytes 14680064 | tf_op jit(solution)/shard_map/dot_general | solution.py:66
  662.0 0.2 constant_dynamic-slice_fusion
  662.2 3.0 collective-permute-start
  665.2 0.7 collective-permute-start.1
  665.9 2.6 pad_maximum_fusion
  668.5 7.8 %psum.22 = f32[4]{0:T(128)S(1)} all-reduce(f32[4]{0:T(128)S(1)} %pad_maximum_fusion), channel_id=1, replica_groups=mesh['row'=8,'col'=4] {'col'}, use_global_device_ids=true, to_apply=%region_6.0 | all-reduce | flops 4 | bytes 32 | tf_op jit(solution)/shard_map/psum | solution.py:77
  676.3 90.5 %psum.23 = f32[4]{0:T(128)S(1)} all-reduce(f32[4]{0:T(128)S(1)} %psum.22), channel_id=1, replica_groups=mesh['row'=8,'col'=4] {'row'}, use_global_device_ids=true, to_apply=%region_7.0 | all-reduce | flops 4 | bytes 32 | tf_op jit(solution)/shard_map/psum | solution.py:77
  766.8 0.5 multiply_sqrt_fusion
  767.3 1.6 copy.3
  768.9 0.3 copy.4
  769.2 0.2 broadcast_in_dim.3
  769.7 1.3 copy-done
  (23 shorter events, 0.6 us)
Async XLA Ops:
  7.2 47.3 %all-gather.10.cloned.1.call-start = ((), (), s32[]{:S(2)}) async-start(), calls=%async_computation | async-start | bytes 5242880 | tf_op jit(solution)/shard_map/all_gather | solution.py:53
  11.5 161.4 %all-gather.12.cloned.1.call-start = ((), (), s32[]{:S(2)}) async-start(), calls=%async_computation.1 | async-start | bytes 9437184 | tf_op jit(solution)/shard_map/all_gather | solution.py:54
  12.3 207.5 %all-gather.14.cloned.1.call-start = ((), (), s32[]{:S(2)}) async-start(), calls=%async_computation.2 | async-start | bytes 5242880 | tf_op jit(solution)/shard_map/all_gather | solution.py:67
  185.1 81.2 %all-gather.16.cloned.1.call-start = ((), (), s32[]{:S(2)}) async-start(), calls=%async_computation.3 | async-start | bytes 5242880 | tf_op jit(solution)/shard_map/all_gather | solution.py:73
  231.7 80.1 %all-gather.18.cloned.1.call-start = ((), (), s32[]{:S(2)}) async-start(), calls=%async_computation.4 | async-start | bytes 5242880 | tf_op jit(solution)/shard_map/all_gather | solution.py:67
  277.2 159.3 %all-gather.20.cloned.1.call-start = ((), (), s32[]{:S(2)}) async-start(), calls=%async_computation.5 | async-start | bytes 9437184 | tf_op jit(solution)/shard_map/all_gather | solution.py:74
  277.8 203.5 %copy-start.1 = (f32[512,1024]{1,0:T(8,128)S(1)}, f32[512,1024]{1,0:T(8,128)}, u32[]{:S(2)}) copy-start(f32[512,1024]{1,0:T(8,128)} %param.1) | copy-start | bytes 6291460
  277.8 203.5 %all-gather.22.cloned.1.call-start = ((), (), s32[]{:S(2)}) async-start(), calls=%async_computation.6 | async-start | bytes 5242880 | tf_op jit(solution)/shard_map/all_gather | solution.py:73
  446.6 82.4 %all-gather.24.cloned.1.call-start = ((), (), s32[]{:S(2)}) async-start(), calls=%async_computation.7 | async-start | bytes 5242880 | tf_op jit(solution)/shard_map/all_gather | solution.py:67
  494.4 159.4 %all-gather.26.cloned.1.call-start = ((), (), s32[]{:S(2)}) async-start(), calls=%async_computation.8 | async-start | bytes 9437184 | tf_op jit(solution)/shard_map/all_gather | solution.py:74
  662.2 105.1 %collective-permute-start = (f32[512,512]{1,0:T(8,128)S(1)}, f32[512,512]{1,0:T(8,128)}, u32[]{:S(2)}, u32[]{:S(2)}) collective-permute-start(f32[512,512]{1,0:T(8,128)S(1)} %get-tuple-element.8), channel_id=1, source_target_pairs={{0,0},{1,8},{2,16},{3,24},{4,4},{5,12},{6,20},{7,28},{8,1},{9,9},{... | collective-permute-start | bytes 3145736 | tf_op jit(solution)/shard_map/ppermute | solution.py:34
  665.2 103.7 %collective-permute-start.1 = (f32[512,512]{1,0:T(8,128)S(1)}, f32[512,512]{1,0:T(8,128)S(1)}, u32[]{:S(2)}, u32[]{:S(2)}) collective-permute-start(f32[512,512]{1,0:T(8,128)S(1)} %get-tuple-element.7), channel_id=1, source_target_pairs={{0,4},{1,12},{2,20},{3,28},{4,0},{5,8},{6,16},{7,24},{8,5},{9,13},... | collective-permute-start | bytes 3145736 | tf_op jit(solution)/shard_map/ppermute | solution.py:34
  769.7 1.3 copy-start
Sparse Core Ops, SparseCore 0:
  11.6 35.8 all-gather.9
  50.2 122.6 all-gather.11
  185.2 34.4 all-gather.13
  231.8 34.4 all-gather.15
  277.3 34.4 all-gather.17
  313.8 122.6 all-gather.19
  446.7 34.4 all-gather.21
  494.5 34.4 all-gather.23
  531.2 122.6 all-gather.25
